TPU v7x, 32 devices: a whole 2x2x4 slice. The times are simulated.
32 devices in a mesh: rows: 8 (over z, x), cols: 4 (over y, core).
Axes of the slice: x: 2, y: 2, z: 4, core: 2. Of those that a mesh axis runs over, the one named last changes fastest.
Arguments:
- basis: float32 [8192, 4096], P('rows', 'cols'), may hold values from -119.66257 to 119.66257, as said below
- block: float32 [8192, 512], P('rows', 'cols'), may hold values from -1800 to 1800
Outputs:
- ortho: float32 [8192, 512], P('rows', 'cols')
- factors: float32 [4, 128, 128], P('cols')
Inputs may be any that keep to these rules, and one draw needn't show every extreme that they name: Under the inner product (sum over rows divided by 8192) the basis columns have squared norms between 0.6 and 1.9, and inner products of distinct basis columns are at most 0.05 in magnitude.
All inputs are finite; a program needn't handle non-finite values.
Results may differ from a plain program's by a relative error of at most 0.000076.
Values sent between devices are 32-bit elements; how exact they have to be, the bound alone decides.
No kernel may reach another device: no remote copies, remote signals or barrier semaphores. Data moves between devices by JAX's collectives and lax.ppermute only.
A program may use at most 64 MiB of HBM per device.

v0:
```python
import jax
import jax.numpy as jnp
from jax import lax
from jax.sharding import PartitionSpec as P

BLK = 128


def solve_block(lower_factor, vectors):
    return jax.scipy.linalg.solve_triangular(lower_factor, vectors, lower=True)


def body(basis, block):
    highest = lax.Precision.HIGHEST
    local_rows = basis.shape[0]
    inverse = 1.0 / (local_rows * lax.axis_size("rows"))
    width = block.shape[1]
    column_index = lax.axis_index("cols")

    def project(piece):
        return (
            lax.dot_general(
                basis,
                piece,
                (((0,), (0,)), ((), ())),
                precision=highest,
                preferred_element_type=jnp.float32,
            )
            * inverse
        )

    def expand(coef):
        return jnp.dot(basis, coef, precision=highest, preferred_element_type=jnp.float32)

    terms_one = project(lax.all_gather(block, "cols", axis=1, tiled=True))
    coef_one = lax.psum(terms_one, "rows")
    placed = lax.dynamic_update_slice_in_dim(
        jnp.zeros((local_rows, coef_one.shape[1]), jnp.float32), block, column_index * width, 1
    )
    first_whole = lax.psum(placed - expand(coef_one), "cols")
    terms_two = project(first_whole)
    first = lax.dynamic_slice_in_dim(first_whole, column_index * width, width, 1)
    coef_two = lax.psum(terms_two, "rows")
    second = first - lax.psum_scatter(expand(coef_two), "cols", scatter_dimension=1, tiled=True)
    blocks = width // BLK
    pieces = second.reshape(local_rows, blocks, BLK)
    gram = jnp.einsum("mbi,mbj->bij", pieces, pieces, precision=highest) * inverse
    gram = lax.psum(gram, "rows")
    lower_factor = jnp.linalg.cholesky(gram)
    solved = jax.vmap(solve_block)(lower_factor, jnp.transpose(pieces, (1, 2, 0)))
    ortho = jnp.transpose(solved, (2, 0, 1)).reshape(local_rows, width)
    return (ortho, jnp.transpose(lower_factor, (0, 2, 1)))


def solution(mesh):
    placed = (P("rows", "cols"), P("rows", "cols"))
    return jax.shard_map(
        body,
        mesh=mesh,
        in_specs=placed,
        out_specs=(P("rows", "cols"), P("cols", None, None)),
        check_vma=False,
    )
```

profile of v0, /device:TPU:0, one launch (start us, length us, event | category | flops | bytes accessed | tf_op | source)
XLA Modules:
  0.0 476.0 jit_solution(7517272405939530119)
XLA Ops:
  7.2 0.7 all-gather.2.cloned.1.call-update
  7.9 27.2 %all-gather.2.cloned.1.call-done = f32[1024,512]{1,0:T(8,128)} async-done(((f32[1024,128]{1,0:T(8,128)}), f32[1024,512]{1,0:T(8,128)}) %all-gather.2.cloned.1.call-update) | async-done | bytes 2097168 | tf_op jit(solution)/shard_map/all_gather | solution.py:35
  35.1 10.2 %convolution_multiply_fusion = f32[1024,512]{1,0:T(8,128)} fusion(f32[1024,1024]{1,0:T(8,128)} %param.2, f32[1024,512]{1,0:T(8,128)} %all-gather.2.cloned.1.call-done), kind=kOutput, calls=%fused_computation.3 | convolution fusion | flops 6442975232 | bytes 8388608 | tf_op jit(solution)/shard_map/dot_general | solution.py:22
  45.4 1.0 copy-done.1
  46.5 0.2 broadcast_in_dim.7
  46.8 100.9 %all-reduce.5.cloned.1.call-done = f32[1024,512]{1,0:T(8,128)} async-done(((f32[1024,512]{1,0:T(8,128)}), f32[1024,512]{1,0:T(8,128)}) %all-reduce.5.cloned.1.call-update) | async-done | bytes 2097168 | tf_op jit(solution)/shard_map/psum | solution.py:36
  147.8 16.7 %bitcast_subtract_fusion = f32[1024,512]{0,1:T(8,128)} fusion(f32[1024,512]{0,1:T(8,128)S(1)} %constant_dynamic-update-slice_fusion, f32[1024,512]{1,0:T(8,128)} %all-reduce.5.cloned.1.call-done, f32[1024,1024]{1,0:T(8,128)} %param.2), kind=kOutput, calls=%fused_computation | convolution fusion | flops 6442975232 | bytes 10485760 | tf_op jit(solution)/shard_map/dot_general | solution.py:33
  164.7 50.6 %all-reduce.7.cloned.1.call-done = f32[1024,512]{0,1:T(8,128)} async-done(((f32[1024,512]{0,1:T(8,128)}), f32[1024,512]{0,1:T(8,128)}) %all-reduce.7.cloned.1.call-update) | async-done | bytes 2097168 | tf_op jit(solution)/shard_map/psum | solution.py:40
  215.3 10.2 %multiply_bitcast_fusion = f32[1024,512]{0,1:T(8,128)} fusion(f32[1024,512]{0,1:T(8,128)} %all-reduce.7.cloned.1.call-done, f32[1024,1024]{1,0:T(8,128)} %param.2), kind=kOutput, calls=%fused_computation.1 | convolution fusion | flops 6442975232 | bytes 8388608 | tf_op jit(solution)/shard_map/dot_general | solution.py:22
  225.6 102.5 %all-reduce.9.cloned.1.call-done = f32[1024,512]{0,1:T(8,128)} async-done(((f32[1024,512]{0,1:T(8,128)}), f32[1024,512]{0,1:T(8,128)}) %all-reduce.9.cloned.1.call-update) | async-done | bytes 2097168 | tf_op jit(solution)/shard_map/psum | solution.py:43
  328.1 10.3 %convolution_bitcast_fusion = f32[1024,512]{0,1:T(8,128)} fusion(f32[1024,512]{0,1:T(8,128)} %all-reduce.9.cloned.1.call-done, f32[1024,1024]{1,0:T(8,128)} %param.2), kind=kOutput, calls=%fused_computation.2 | convolution fusion | flops 6442450944 | bytes 8388608 | tf_op jit(solution)/shard_map/dot_general | solution.py:33
  338.4 0.3 all-reduce.11.cloned.1.call-start
  338.7 30.3 %reduce-scatter.2.cloned.1.call-done = f32[1024,128]{0,1:T(8,128)} async-done(((f32[1024,512]{0,1:T(8,128)}), f32[1024,128]{0,1:T(8,128)}) %reduce-scatter.2.cloned.1.call-update) | async-done | bytes 524304 | tf_op jit(solution)/shard_map/reduce_scatter | solution.py:44
  369.0 2.5 fusion
  371.5 70.6 %all-reduce.11.cloned.1.call-done = f32[1,128,128]{1,2,0:T(8,128)} async-done(((f32[1,128,128]{1,2,0:T(8,128)}), f32[1,128,128]{1,2,0:T(8,128)}) %all-reduce.11.cloned.1.call-update) | async-done | bytes 65552 | tf_op jit(solution)/shard_map/psum | solution.py:48
  442.2 0.9 copy.6
  443.1 0.9 fusion.3
  444.0 11.7 %custom-call.8 = f32[1,128,128]{2,1,0:T(8,128)S(1)} custom-call(f32[1,128,128]{2,1,0:T(8,128)S(1)} %fusion.3), custom_call_target="Cholesky" | custom-call | tf_op jit(solution)/shard_map/jit(cholesky)/cholesky | solution.py:49
  455.7 0.6 compare_reduce_fusion
  456.4 0.7 fusion.4
  457.0 9.8 %custom-call.9 = f32[1,1,128,128]{2,3,1,0:T(8,128)S(1)} custom-call(f32[1,1,128,128]{3,2,1,0:T(8,128)S(1)} %get-tuple-element.5), custom_call_target="InvertDiagBlocksLowerTriangular" | custom-call | tf_op jit(solution)/shard_map/vmap(jit(_solve_triangular))/triangular_solve | solution.py:10
  466.8 0.6 convolution_bitcast_fusion.1
  467.5 1.0 copy.7
  468.5 0.7 copy.8
  (18 shorter events, 0.8 us)
Async XLA Ops:
  7.2 27.9 %all-gather.2.cloned.1.call-start = ((), (), s32[]{:S(2)}) async-start(), calls=%async_computation.1 | async-start | bytes 2621440 | tf_op jit(solution)/shard_map/all_gather | solution.py:35
  7.9 139.9 %all-reduce.5.cloned.1.call-start = ((), (), s32[]{:S(2)}) async-start(), calls=%async_computation.2 | async-start | bytes 4194304 | tf_op jit(solution)/shard_map/psum | solution.py:36
  45.3 1.0 copy-start.1
  45.3 170.0 %all-reduce.7.cloned.1.call-start = ((), (), s32[]{:S(2)}) async-start(), calls=%async_computation.3 | async-start | bytes 4194304 | tf_op jit(solution)/shard_map/psum | solution.py:40
  164.5 163.6 %all-reduce.9.cloned.1.call-start = ((), (), s32[]{:S(2)}) async-start(), calls=%async_computation.4 | async-start | bytes 4194304 | tf_op jit(solution)/shard_map/psum | solution.py:43
  225.6 143.4 %reduce-scatter.2.cloned.1.call-start = ((), (), s32[]{:S(2)}) async-start(), calls=%async_computation.5 | async-start | bytes 2621440 | tf_op jit(solution)/shard_map/reduce_scatter | solution.py:44
  338.4 30.6 %copy-start = (f32[1024,512]{0,1:T(8,128)S(1)}, f32[1024,512]{0,1:T(8,128)}, u32[]{:S(2)}) copy-start(f32[1024,512]{0,1:T(8,128)} %all-reduce.7.cloned.1.call-done) | copy-start | bytes 6291460
  338.4 103.8 %all-reduce.11.cloned.1.call-start = ((), (), s32[]{:S(2)}) async-start(), calls=%async_computation.6 | async-start | bytes 131072 | tf_op jit(solution)/shard_map/psum | solution.py:48
  369.0 97.8 %copy-start.2 = (f32[1024,128]{0,1:T(8,128)S(1)}, f32[1024,128]{0,1:T(8,128)}, u32[]{:S(2)}) copy-start(f32[1024,128]{0,1:T(8,128)} %reduce-scatter.2.cloned.1.call-done) | copy-start | bytes 1572868
Sparse Core Ops, SparseCore 0:
  9.5 25.5 all-gather.1
  45.4 102.3 all-reduce.4
  164.6 50.6 all-reduce.6
  225.7 102.3 all-reduce.8
  338.5 30.4 reduce-scatter.1
  372.9 69.2 all-reduce.10
where the time goes:
time: 476 us
  waiting for transfers between devices  383 us (80%)
  matrix products  50.5 us (11%)
  other arithmetic  23.7 us (5%)
  between operations  14.2 us (3%)
    psum x1, waiting for transfers between devices, body(): coef_two = lax.psum(terms_two, 'rows')  102 us
    psum x1, waiting for transfers between devices, body(): coef_one = lax.psum(terms_one, 'rows')  101 us
    psum x1, waiting for transfers between devices, body(): gram = lax.psum(gram, 'rows')  70.6 us
    psum x1, waiting for transfers between devices, body(): first_whole = lax.psum(placed - expand(coef_one), 'cols')  50.6 us
    reduce_scatter x1, waiting for transfers between devices, body(): lax.psum_scatter(expand(coef_two), 'cols', scatter_dimension=1, tiled=True)  30.3 us
    all_gather x1, waiting for transfers between devices, body(): terms_one = project(lax.all_gather(block, 'cols', axis=1, tiled=True))  27.2 us
    dot_general x2, matrix products, expand(): jnp.dot(basis, coef, precision=highest, preferred_element_type=jnp.float32)  27 us
    dot_general x2, matrix products, project(): lax.dot_general(basis, piece, (((0,), (0,)), ((), ())), precision=highest...  20.4 us
  transfers between devices with their start and end apart: 6, of which 6 were waited for; matrix products, arithmetic and copies ran while one was open for 0% of the time, Pallas kernels for 0%

commit v1 on v0

--- a/solution.py
+++ b/solution.py
@@ -37,7 +37,9 @@
     placed = lax.dynamic_update_slice_in_dim(
         jnp.zeros((local_rows, coef_one.shape[1]), jnp.float32), block, column_index * width, 1
     )
-    first_whole = lax.psum(placed - expand(coef_one), "cols")
+    part = placed - expand(coef_one)
+    parts = lax.all_gather(part, "cols")
+    first_whole = jnp.sum(parts, axis=0)
     terms_two = project(first_whole)
     first = lax.dynamic_slice_in_dim(first_whole, column_index * width, width, 1)
     coef_two = lax.psum(terms_two, "rows")

time: 476 us -> 502 us (1.055)
  local copies, waits for them, and re-layouts: 4.11 us -> 14.9 us
  other arithmetic: 23.7 us -> 32.2 us
  waiting for transfers between devices: 383 us -> 390 us
    all_gather x0 -> x1, waiting for transfers between devices: none -> 57.5 us  [body(): parts = lax.all_gather(part, 'cols')]
    psum x1 -> x0, waiting for transfers between devices: 50.6 us -> none  [body(): first_whole = lax.psum(placed - expand(coef_one), 'cols')]
    all_gather x0 -> x1, local copies, waits for them, and re-layouts: none -> 10.8 us  [body(): parts = lax.all_gather(part, 'cols')]
    reduce_sum x0 -> x1, other arithmetic: none -> 8.49 us  [body(): first_whole = jnp.sum(parts, axis=0)]
where the time goes in v1:
time: 502 us
  waiting for transfers between devices  390 us (78%)
  matrix products  49.9 us (10%)
  other arithmetic  32.2 us (6%)
  local copies, waits for them, and re-layouts  14.9 us (3%)
  between operations  14.2 us (3%)
    psum x1, waiting for transfers between devices, body(): coef_two = lax.psum(terms_two, 'rows')  102 us
    psum x1, waiting for transfers between devices, body(): coef_one = lax.psum(terms_one, 'rows')  101 us
    psum x1, waiting for transfers between devices, body(): gram = lax.psum(gram, 'rows')  70.6 us
    all_gather x1, waiting for transfers between devices, body(): parts = lax.all_gather(part, 'cols')  57.5 us
    reduce_scatter x1, waiting for transfers between devices, body(): lax.psum_scatter(expand(coef_two), 'cols', scatter_dimension=1, tiled=True)  30.6 us
    all_gather x1, waiting for transfers between devices, body(): terms_one = project(lax.all_gather(block, 'cols', axis=1, tiled=True))  27.2 us
    dot_general x2, matrix products, expand(): jnp.dot(basis, coef, precision=highest, preferred_element_type=jnp.float32)  27 us
    dot_general x2, matrix products, project(): lax.dot_general(basis, piece, (((0,), (0,)), ((), ())), precision=highest...  19.8 us
  transfers between devices with their start and end apart: 6, of which 6 were waited for; matrix products, arithmetic and copies ran while one was open for 0% of the time, Pallas kernels for 0%

profile of v1, /device:TPU:0, one launch (start us, length us, event | category | flops | bytes accessed | tf_op | source)
XLA Modules:
  0.0 501.5 jit_solution(5086193454067057085)
XLA Ops:
  7.2 0.7 all-gather.4.cloned.1.call-update
  7.9 27.2 %all-gather.4.cloned.1.call-done = f32[1024,512]{1,0:T(8,128)} async-done(((f32[1024,128]{1,0:T(8,128)}), f32[1024,512]{1,0:T(8,128)}) %all-gather.4.cloned.1.call-update) | async-done | bytes 2097168 | tf_op jit(solution)/shard_map/all_gather | solution.py:35
  35.1 10.2 %convolution_multiply_fusion = f32[1024,512]{1,0:T(8,128)} fusion(f32[1024,1024]{1,0:T(8,128)} %param.2, f32[1024,512]{1,0:T(8,128)} %all-gather.4.cloned.1.call-done), kind=kOutput, calls=%fused_computation.3 | convolution fusion | flops 6442975232 | bytes 8388608 | tf_op jit(solution)/shard_map/dot_general | solution.py:22
  45.4 1.0 copy-done
  46.9 100.9 %all-reduce.4.cloned.1.call-done = f32[1024,512]{1,0:T(8,128)} async-done(((f32[1024,512]{1,0:T(8,128)}), f32[1024,512]{1,0:T(8,128)}) %all-reduce.4.cloned.1.call-update) | async-done | bytes 2097168 | tf_op jit(solution)/shard_map/psum | solution.py:36
  147.8 16.7 %bitcast_subtract_fusion = f32[1024,512]{0,1:T(8,128)} fusion(f32[1024,512]{0,1:T(8,128)S(1)} %constant_dynamic-update-slice_fusion, f32[1024,512]{1,0:T(8,128)} %all-reduce.4.cloned.1.call-done, f32[1024,1024]{1,0:T(8,128)} %param.2), kind=kOutput, calls=%fused_computation | convolution fusion | flops 6442975232 | bytes 10485760 | tf_op jit(solution)/shard_map/dot_general | solution.py:33
  164.7 57.5 %all-gather.6.cloned.1.call-done = f32[4096,512]{0,1:T(8,128)} async-done(((f32[1024,512]{0,1:T(8,128)}), f32[4096,512]{0,1:T(8,128)}) %all-gather.6.cloned.1.call-update) | async-done | bytes 8388624 | tf_op jit(solution)/shard_map/all_gather | solution.py:41
  222.2 10.8 %reshape.74 = f32[4,1024,512]{1,0,2:T(4,128)} reshape(f32[4096,512]{0,1:T(8,128)} %all-gather.6.cloned.1.call-done) | data formatting | bytes 16777216 | tf_op jit(solution)/shard_map/all_gather | solution.py:41
  233.0 8.5 %reduce_sum.9 = f32[1024,512]{0,1:T(8,128)S(1)} reduce(f32[4,1024,512]{1,0,2:T(4,128)} %reshape.74, f32[]{:T(128)} %constant.52.clone.1), dimensions={0}, to_apply=%region_1.0 | reduce | flops 1572864 | bytes 10485764 | tf_op jit(solution)/shard_map/reduce_sum | solution.py:42
  241.5 9.6 %multiply_bitcast_fusion = f32[1024,512]{0,1:T(8,128)} fusion(f32[1024,512]{0,1:T(8,128)S(1)} %reduce_sum.9, f32[1024,1024]{1,0:T(8,128)} %param.2), kind=kOutput, calls=%fused_computation.1 | convolution fusion | flops 6442975232 | bytes 8388608 | tf_op jit(solution)/shard_map/dot_general | solution.py:22
  251.4 102.2 %all-reduce.6.cloned.1.call-done = f32[1024,512]{0,1:T(8,128)} async-done(((f32[1024,512]{0,1:T(8,128)}), f32[1024,512]{0,1:T(8,128)}) %all-reduce.6.cloned.1.call-update) | async-done | bytes 2097168 | tf_op jit(solution)/shard_map/psum | solution.py:45
  353.6 10.3 %convolution_bitcast_fusion = f32[1024,512]{0,1:T(8,128)} fusion(f32[1024,512]{0,1:T(8,128)} %all-reduce.6.cloned.1.call-done, f32[1024,1024]{1,0:T(8,128)} %param.2), kind=kOutput, calls=%fused_computation.2 | convolution fusion | flops 6442450944 | bytes 8388608 | tf_op jit(solution)/shard_map/dot_general | solution.py:33
  364.0 30.6 %reduce-scatter.2.cloned.1.call-done = f32[1024,128]{0,1:T(8,128)} async-done(((f32[1024,512]{0,1:T(8,128)}), f32[1024,128]{0,1:T(8,128)}) %reduce-scatter.2.cloned.1.call-update) | async-done | bytes 524304 | tf_op jit(solution)/shard_map/reduce_scatter | solution.py:46
  394.5 2.5 fusion
  397.1 70.6 %all-reduce.8.cloned.1.call-done = f32[1,128,128]{1,2,0:T(8,128)} async-done(((f32[1,128,128]{1,2,0:T(8,128)}), f32[1,128,128]{1,2,0:T(8,128)}) %all-reduce.8.cloned.1.call-update) | async-done | bytes 65552 | tf_op jit(solution)/shard_map/psum | solution.py:50
  467.7 0.9 copy.6
  468.6 0.9 fusion.3
  469.5 11.7 %custom-call.8 = f32[1,128,128]{2,1,0:T(8,128)S(1)} custom-call(f32[1,128,128]{2,1,0:T(8,128)S(1)} %fusion.3), custom_call_target="Cholesky" | custom-call | tf_op jit(solution)/shard_map/jit(cholesky)/cholesky | solution.py:51
  481.2 0.6 compare_reduce_fusion
  481.8 0.7 fusion.4
  482.5 0.7 copy.8
  483.2 9.8 %custom-call.9 = f32[1,1,128,128]{2,3,1,0:T(8,128)S(1)} custom-call(f32[1,1,128,128]{3,2,1,0:T(8,128)S(1)} %get-tuple-element.5), custom_call_target="InvertDiagBlocksLowerTriangular" | custom-call | tf_op jit(solution)/shard_map/vmap(jit(_solve_triangular))/triangular_solve | solution.py:10
  493.1 0.6 convolution_bitcast_fusion.1
  493.7 1.0 copy.7
  (18 shorter events, 1.3 us)
Async XLA Ops:
  7.2 27.9 %all-gather.4.cloned.1.call-start = ((), (), s32[]{:S(2)}) async-start(), calls=%async_computation.1 | async-start | bytes 2621440 | tf_op jit(solution)/shard_map/all_gather | solution.py:35
  7.9 139.9 %all-reduce.4.cloned.1.call-start = ((), (), s32[]{:S(2)}) async-start(), calls=%async_computation.2 | async-start | bytes 4194304 | tf_op jit(solution)/shard_map/psum | solution.py:36
  45.3 1.0 copy-start
  45.3 176.9 %all-gather.6.cloned.1.call-start = ((), (), s32[]{:S(2)}) async-start(), calls=%async_computation.6 | async-start | bytes 10485760 | tf_op jit(solution)/shard_map/all_gather | solution.py:41
  164.5 189.1 %all-reduce.6.cloned.1.call-start = ((), (), s32[]{:S(2)}) async-start(), calls=%async_computation.3 | async-start | bytes 4194304 | tf_op jit(solution)/shard_map/psum | solution.py:45
  251.2 143.4 %reduce-scatter.2.cloned.1.call-start = ((), (), s32[]{:S(2)}) async-start(), calls=%async_computation.4 | async-start | bytes 2621440 | tf_op jit(solution)/shard_map/reduce_scatter | solution.py:46
  363.9 103.7 %all-reduce.8.cloned.1.call-start = ((), (), s32[]{:S(2)}) async-start(), calls=%async_computation.5 | async-start | bytes 131072 | tf_op jit(solution)/shard_map/psum | solution.py:50
  394.5 98.5 %copy-start.1 = (f32[1024,128]{0,1:T(8,128)S(1)}, f32[1024,128]{0,1:T(8,128)}, u32[]{:S(2)}) copy-start(f32[1024,128]{0,1:T(8,128)} %reduce-scatter.2.cloned.1.call-done) | copy-start | bytes 1572868
Sparse Core Ops, SparseCore 0:
  9.5 25.5 all-gather.3
  45.4 102.3 all-reduce.3
  164.6 57.5 all-gather.5
  251.3 102.2 all-reduce.5
  364.1 30.4 reduce-scatter.1
  398.4 69.2 all-reduce.7
